TPU v7x, 32 devices: a whole 2x2x4 slice. The times are simulated.
32 devices in a mesh: leaf: 32 (over z, y, x, core).
Axes of the slice: x: 2, y: 2, z: 4, core: 2. Of those that a mesh axis runs over, the one named last changes fastest.
Arguments:
- shots: float32 [32768, 2048], P('leaf'), may hold values from -6 to 6
- leaf_inverse: float32 [32768, 1024], P('leaf'), may hold values from -0.1875 to 0.1875
- leaf_basis: float32 [8192, 1024], P('leaf'), may hold values from -0.1875 to 0.1875
- leaf_back: float32 [32768, 256], P('leaf'), may hold values from -0.375 to 0.375
- level_one: float32 [8192, 1024], P('leaf'), may hold values from -0.25 to 0.25
- level_two: float32 [4096, 1024], P('leaf'), may hold values from -0.25 to 0.25
- level_three: float32 [2048, 1024], P('leaf'), may hold values from -0.25 to 0.25
- top_inverse: float32 [1024, 1024], P('leaf'), may hold values from -0.1 to 0.1, as said below
Outputs:
- solution: float32 [32768, 2048], P('leaf')
Inputs may be any that keep to these rules, and one draw needn't show every extreme that they name: top_inverse is symmetric.
All inputs are finite; a program needn't handle non-finite values.
Results may differ from a plain program's by a relative error of at most 0.0001.
Values sent between devices are 32-bit elements; how exact they have to be, the bound alone decides.
A program may use at most 128 MiB of HBM per device.

v0:
```python
import functools

import jax
import jax.numpy as jnp
from jax import lax
from jax.experimental import pallas as pl
from jax.experimental.pallas import tpu as pltpu
from jax.sharding import PartitionSpec as P

LEVELS = 3
CHUNKS = 2
DEPTHS = 2
HIGH = lax.Precision.HIGH
MESH = pl.DeviceIdType.MESH
VMEM_LIMIT = 48 * 2**20


def dot(a, b):
    return jnp.dot(a, b, precision=HIGH, preferred_element_type=jnp.float32)


def dot_t(a, b):
    dims = (((0,), (0,)), ((), ()))
    return lax.dot_general(a, b, dims, precision=HIGH, preferred_element_type=jnp.float32)


def halves(rows):
    return [pl.ds(i * (rows // 2), rows // 2) for i in range(2)]


def product(dst, a, b, minus=None):
    for rows in halves(dst.shape[0]):
        term = dot(a[rows], b)
        dst[rows, :] = term if minus is None else minus[rows, :] - term


def solve_kernel(
    sizes,
    shots, leaf_inverse, leaf_basis, leaf_back, level_one, level_two, level_three, top_inverse,
    out, w0,
    b, e, p, h, f1, f2, f3, top, a0, g1, g2, g3,
    c0send, c0, c1send, c1, c2send, c2, call,
    z1, z2, z3, w3, w2send, w2, w1send, w1, w0send,
    local_sem, send_sem, recv_sem, z_send, z_recv,
):
    n, rank, nodes = sizes
    lanes1 = b.shape[3]
    lanes2, lanes3 = lanes1 // 2, lanes1 // 4
    me = lax.axis_index("leaf")
    core, x, y, z = me % 2, me // 2 % 2, me // 4 % 2, me // 8
    to_core = me + 1 - 2 * core
    to_x = me + 2 - 4 * x
    to_y = me + 4 - 8 * y
    to_z = {k: me + 8 * (flip_of(z, k) - z) for k in range(1, nodes)}
    inner = (z % 4 == 1) | (z % 4 == 2)
    def ds(index, size):
        return pl.ds(pl.multiple_of(index * size, size), size)

    count = [0]
    local = {}

    def load(name, src, dst):
        local[name] = pltpu.make_async_copy(src, dst, local_sem.at[len(local)])
        local[name].start()

    remote = {}

    def send(name, src, dst, to):
        prepare(name, src, dst, to)
        remote[name].start()

    def prepare(name, src, dst, to):
        i = len(remote)
        remote[name] = pltpu.make_async_remote_copy(
            src_ref=src, dst_ref=dst, send_sem=send_sem.at[i], recv_sem=recv_sem.at[i],
            device_id=(to,), device_id_type=MESH,
        )

    def arrived(name):
        remote[name].wait_recv()

    def columns(c, side):
        half = core if side == 0 else 1 - core
        return ds(c * 2 + half, lanes1)

    load("p", leaf_basis, p)
    load("e", leaf_inverse, e)
    load("b01", shots.at[:, columns(0, 1)], b.at[0, 1])
    load("b00", shots.at[:, columns(0, 0)], b.at[0, 0])
    rows1, rows2, rows3, rows4 = (r.shape[0] for r in (level_one, level_two, level_three, top_inverse))
    slot2, slot3 = x * 2 + core, y * 4 + x * 2 + core
    load("f1", level_one, f1.at[ds(core, rows1)])
    load("b11", shots.at[:, columns(1, 1)], b.at[1, 1])
    load("b10", shots.at[:, columns(1, 0)], b.at[1, 0])
    load("f2", level_two, f2.at[ds(slot2, rows2)])
    load("f3", level_three, f3.at[ds(slot3, rows3)])
    load("top", top_inverse, top.at[ds(slot3, rows4)])
    load("h", leaf_back, h)

    barrier = pltpu.get_barrier_semaphore()

    def between(k):
        return inner if k == 3 else None

    def guarded(condition, action):
        action() if condition is None else pl.when(condition)(action)

    def greet(peer):
        pl.semaphore_signal(barrier, inc=1, device_id=(peer,), device_id_type=MESH)

    for peer in (to_core, to_x, to_y):
        greet(peer)
    for k, peer in to_z.items():
        guarded(between(k), functools.partial(greet, peer))
    far = 1 - inner.astype(jnp.int32) if nodes > 3 else 0
    pl.semaphore_wait(barrier, 3 + len(to_z) - far)

    kq, fc = pl.ds(0, 3 * rank), pl.ds(3 * rank, rank)
    slot2x = (1 - x) * 2 + core
    slot3x, slot3y = y * 4 + (1 - x) * 2 + core, (1 - y) * 4 + x * 2 + core
    slot3xy = (1 - y) * 4 + (1 - x) * 2 + core
    send("f1", level_one, f1.at[ds(core, rows1)], to_core)
    send("f3y", level_three.at[:, kq], f3.at[ds(slot3, rows3), kq], to_y)
    send("f3x", level_three.at[:, kq], f3.at[ds(slot3, rows3), kq], to_x)
    send("f2x", level_two.at[:, kq], f2.at[ds(slot2, rows2), kq], to_x)
    send("f2c", level_two, f2.at[ds(slot2, rows2)], to_core)
    send("f3c", level_three, f3.at[ds(slot3, rows3)], to_core)
    send("tc", top_inverse, top.at[ds(slot3, rows4)], to_core)

    def forward(name, buf, slot, rows, cols, to):
        view = buf.at[ds(slot, rows), cols]
        send(name, view, view, to)

    cols4 = pl.ds(0, top.shape[1])
    share = ((top, rows4, cols4), (f3, rows3, fc))
    for name, (buf, rows, cols) in zip(("t", "f"), share):
        src = top_inverse if name == "t" else level_three.at[:, fc]
        prepare(name + "x", src, buf.at[ds(slot3, rows), cols], to_x)
        view = buf.at[ds(slot3x, rows), cols]
        prepare(name + "xy", view, view, to_y)
        prepare(name + "xc", view, view, to_core)

    def forward_late():
        for name in "tf":
            remote[name + "x"].wait_recv()
            remote[name + "xy"].start()
            remote[name + "xc"].start()

    local["p"].wait()
    local["e"].wait()
    a0[...] = dot(p[...], e[...])
    for c in range(CHUNKS):
        local[f"b{c}1"].wait()
        c0send[c] = dot(a0[...], b[c, 1])
        send(f"c0_{c}", c0send.at[c], c0.at[c, ds(core, rank)], to_core)
        local[f"b{c}0"].wait()
        c0[c, ds(core, rank), :] = dot(a0[...], b[c, 0])

    def pieces(first, last):
        def piece(i, carry):
            i, part = i // DEPTHS, i % DEPTHS
            rows = pl.ds(pl.multiple_of(i % 2 * half_leaf, half_leaf), half_leaf)
            depth = ds(part, e.shape[1] // DEPTHS)
            c, side = i // 4, i // 2 % 2
            total = jnp.where(part == 0, 0.0, out[c, side, rows, :])
            out[c, side, rows, :] = total + dot(e[rows, depth], b[c, side, depth, :])
            return carry

        lax.fori_loop(DEPTHS * first, DEPTHS * last, piece, 0)

    half_leaf = e.shape[0] // 2

    def z1_piece(c):
        z1[c] = dot(f1[:, : 2 * rank], c0[c])

    local["f1"].wait()
    arrived("f1")
    g1[...] = dot_t(f1[:, 2 * rank : 3 * rank], f1[:, : 2 * rank])
    pieces(0, core)
    arrived("f3x")
    forward("f3xy", f3, slot3x, rows3, kq, to_y)
    forward("f3xc", f3, slot3x, rows3, kq, to_core)
    arrived("f3y")
    forward("f3yc", f3, slot3y, rows3, kq, to_core)
    send("ty", top_inverse, top.at[ds(slot3, rows4)], to_y)
    send("f3fy", level_three.at[:, fc], f3.at[ds(slot3, rows3), fc], to_y)
    pieces(core, 4 * core)
    for c in range(CHUNKS):
        arrived(f"c0_{c}")
        product(c1send.at[c], g1, c0[c, :, ds(1 - x, lanes2)])
        for part, half in enumerate((1 - y, y)):
            cols = ds(half, lanes3)
            send(f"c1_{c}{part}", c1send.at[c, :, cols], c1.at[c, ds(x, rank), cols], to_x)
        if c == 0:
            remote["tx"].start()
            remote["fx"].start()
        product(c1.at[c, ds(x, rank)], g1, c0[c, :, ds(x, lanes2)])
    send("f2fx", level_two.at[:, fc], f2.at[ds(slot2, rows2), fc], to_x)

    pieces(4 * core, 3 + core)
    arrived("f3xy")
    forward("f3xyc", f3, slot3xy, rows3, kq, to_core)
    arrived("f2x")
    forward("f2xc", f2, slot2x, rows2, kq, to_core)
    z1_piece(0)
    local["f3"].wait()
    for name in ("f3c", "f3yc", "f3xc", "f3xyc"):
        arrived(name)
    g3[...] = dot_t(f3[:, 2 * rank : 3 * rank], f3[:, : 2 * rank])
    local["f2"].wait()
    arrived("f2c")
    arrived("f2xc")
    g2[...] = dot_t(f2[:, 2 * rank : 3 * rank], f2[:, : 2 * rank])

    def up_two(c, part):
        arrived(f"c1_{c}{part}")
        if part == 0:
            cols = ds(1 - y, lanes3)
            product(c2send.at[c], g2, c1[c, :, cols])
            send(f"c2_{c}", c2send.at[c], c2.at[c, ds(y, rank)], to_y)
        else:
            product(c2.at[c, ds(y, rank)], g2, c1[c, :, ds(y, lanes3)])

    def up_three(c):
        arrived(f"c2_{c}")
        product(call.at[c, ds(z, rank)], g3, c2[c])
        for k in sorted(to_z, key=lambda k: (k != 2, -k)):
            guarded(between(k), block(c, k).start)

    def block(c, k):
        view = call.at[c, ds(z, rank)]
        i = c * nodes + k
        return pltpu.make_async_remote_copy(
            src_ref=view, dst_ref=view, send_sem=z_send.at[i], recv_sem=z_recv.at[i],
            device_id=(to_z[k],), device_id_type=MESH,
        )

    def passed(c):
        view = call.at[c, ds(flip_of(z, 2), rank)]
        return pltpu.make_async_remote_copy(
            src_ref=view, dst_ref=view, send_sem=z_send.at[c * nodes], recv_sem=z_recv.at[c * nodes + 3],
            device_id=(to_z[1],), device_id_type=MESH,
        )

    def pass_on(c):
        if nodes > 3:
            @pl.when(inner)
            def _():
                block(c, 2).wait_recv()
                passed(c).start()

    def gathered(c):
        for k in to_z:
            guarded(~inner if k == 2 and nodes > 3 else None, block(c, k).wait_recv)

    up_two(0, 0)
    pieces(4 * core, 5 * core)
    up_two(0, 1)
    product(z2.at[0], f2.at[:, : 2 * rank], c1[0])
    arrived("ty")
    forward("tyc", top, slot3y, rows4, cols4, to_core)
    arrived("f3fy")
    forward("f3fyc", f3, slot3y, rows3, fc, to_core)
    pieces(3 + 2 * core, 4 + core)
    up_three(0)
    forward_late()
    product(z3.at[0], f3.at[:, : 2 * rank], c2[0])
    pieces(4 + core, 5 + core)
    up_two(1, 0)
    z1_piece(1)
    arrived("txy")
    forward("txyc", top, slot3xy, rows4, cols4, to_core)
    arrived("fxy")
    forward("fxyc", f3, slot3xy, rows3, fc, to_core)
    up_two(1, 1)
    pass_on(0)
    up_three(1)
    product(z3.at[1], f3.at[:, : 2 * rank], c2[1])
    pieces(5 + core, 6)
    product(z2.at[1], f2.at[:, : 2 * rank], c1[1])
    local["top"].wait()
    for name in ("tc", "tyc", "txc", "txyc", "f3fyc", "fxc", "fxyc"):
        arrived(name)

    def down_three(c):
        gathered(c)
        product(w3, top, call[c])
        other = pl.ds(pl.multiple_of((1 - y) * rank, rank), rank)
        own = pl.ds(pl.multiple_of(y * rank, rank), rank)
        product(w2send.at[c], f3.at[other, 3 * rank :], w3[...], z3.at[c, other])
        send(f"w2_{c}", w2send.at[c], w2.at[c, :, ds(y, lanes3)], to_y)
        product(w2.at[c, :, ds(y, lanes3)], f3.at[own, 3 * rank :], w3[...], z3.at[c, own])

    def down_two(c, part):
        half = y if part == 0 else 1 - y
        if part == 1:
            arrived(f"w2_{c}")
        cols = ds(half, lanes3)
        lanes = pl.ds(pl.multiple_of(x * lanes2 + half * lanes3, lanes3), lanes3)
        other = pl.ds(pl.multiple_of((1 - x) * rank, rank), rank)
        own = pl.ds(pl.multiple_of(x * rank, rank), rank)
        product(w1send.at[c, :, cols], f2.at[other, 3 * rank :], w2[c, :, cols], z2.at[c, other, cols])
        send(f"w1_{c}{part}", w1send.at[c, :, cols], w1.at[c, :, lanes], to_x)
        product(w1.at[c, :, lanes], f2.at[own, 3 * rank :], w2[c, :, cols], z2.at[c, own, cols])

    def down_one(c, part):
        half = x if part == 0 else 1 - x
        if part == 1:
            arrived(f"w1_{c}0")
            arrived(f"w1_{c}1")
        lanes = ds(half, lanes2)
        other = pl.ds(pl.multiple_of((1 - core) * rank, rank), rank)
        own = pl.ds(pl.multiple_of(core * rank, rank), rank)
        product(w0send.at[c, :, lanes], f1.at[other, 3 * rank :], w1[c, :, lanes], z1.at[c, other, lanes])
        send(f"w0_{c}{part}", w0send.at[c, :, lanes], w0.at[c, 1, :, lanes], to_core)
        product(w0.at[c, 0, :, lanes], f1.at[own, 3 * rank :], w1[c, :, lanes], z1.at[c, own, lanes])

    def last(c, side, half):
        lanes = ds(half, lanes2)
        product(out.at[c, side, :, lanes], h, w0[c, side, :, lanes], out.at[c, side, :, lanes])

    down_three(0)
    arrived("f2fx")
    forward("f2fxc", f2, slot2x, rows2, fc, to_core)
    pieces(6, 7)
    arrived("f2fxc")
    down_two(0, 0)
    pass_on(1)
    down_two(0, 1)
    down_one(0, 0)
    pieces(7, 8)
    down_three(1)
    down_two(1, 0)
    down_one(0, 1)
    local["h"].wait()
    last(0, 0, x)
    down_two(1, 1)
    down_one(1, 0)
    last(0, 0, 1 - x)
    arrived("w0_00")
    last(0, 1, x)
    last(1, 0, x)
    arrived("w0_10")
    last(1, 1, x)
    arrived("w0_01")
    last(0, 1, 1 - x)
    down_one(1, 1)
    last(1, 0, 1 - x)
    arrived("w0_11")
    for copy in remote.values():
        copy.wait_send()
    for c in range(CHUNKS):
        for k in to_z:
            guarded(between(k), block(c, k).wait_send)
        if nodes > 3:
            pl.when(inner)(passed(c).wait_send)


def flip_of(value, mask):
    bit = 1
    while bit <= mask:
        if mask & bit:
            value = value + bit - 2 * bit * (value // bit % 2)
        bit *= 2
    return value


def finish_kernel(part, w0, h, out, done, sem):
    me = lax.axis_index("leaf")
    core, x = me % 2, me // 2 % 2
    lanes1 = part.shape[3]
    lanes2 = lanes1 // 2
    copies = []

    def columns(c, side, half):
        start = c * 4 + (core if side == 0 else 1 - core) * 2 + half
        return pl.ds(pl.multiple_of(start * lanes2, lanes2), lanes2)

    def store(src, cols):
        copies.append(pltpu.make_async_copy(src, out.at[:, cols], sem.at[len(copies)]))
        copies[-1].start()

    for c in range(CHUNKS):
        for side in range(2):
            for half in (x, 1 - x):
                lanes = pl.ds(pl.multiple_of(half * lanes2, lanes2), lanes2)
                if len(copies) < 4 * CHUNKS - 1:
                    store(part.at[c, side, :, lanes], columns(c, side, half))
    for rows in halves(done.shape[0]):
        done[rows, :] = part[1, 1, rows, lanes] - dot(h[rows, :], w0[1, 1, :, lanes])
    store(done, columns(c, side, half))
    for copy in copies:
        copy.wait()


def shards(n, *args):
    shots, leaf_inverse, leaf_basis, leaf_back, level_one, level_two, level_three, top_inverse = args
    rank, rows = leaf_basis.shape
    nodes = n // 2**LEVELS
    width = shots.shape[1] // CHUNKS
    l1, l2, l3 = width // 2, width // 4, width // 8
    f32 = jnp.float32
    vmem = lambda *shape: pltpu.VMEM(shape, f32)
    z_count = CHUNKS * nodes
    part, w0 = pl.pallas_call(
        functools.partial(solve_kernel, (n, rank, nodes)),
        name="solve",
        out_shape=(
            pltpu.VMEM((CHUNKS, 2, rows, l1), f32),
            pltpu.VMEM((CHUNKS, 2, rank, l1), f32),
        ),
        in_specs=[pl.BlockSpec(memory_space=pl.ANY)] * 8,
        out_specs=[pl.BlockSpec(memory_space=pltpu.VMEM)] * 2,
        scratch_shapes=[
            vmem(CHUNKS, 2, rows, l1),
            vmem(*leaf_inverse.shape),
            vmem(*leaf_basis.shape),
            vmem(*leaf_back.shape),
            vmem(2 * rank, 4 * rank),
            vmem(2 * rank, 4 * rank),
            vmem(2 * rank, 4 * rank),
            vmem(rank, nodes * rank),
            vmem(rank, rows),
            vmem(rank, 2 * rank),
            vmem(rank, 2 * rank),
            vmem(rank, 2 * rank),
            vmem(CHUNKS, rank, l1),
            vmem(CHUNKS, 2 * rank, l1),
            vmem(CHUNKS, rank, l2),
            vmem(CHUNKS, 2 * rank, l2),
            vmem(CHUNKS, rank, l3),
            vmem(CHUNKS, 2 * rank, l3),
            vmem(CHUNKS, nodes * rank, l3),
            vmem(CHUNKS, 2 * rank, l1),
            vmem(CHUNKS, 2 * rank, l2),
            vmem(CHUNKS, 2 * rank, l3),
            vmem(rank, l3),
            vmem(CHUNKS, rank, l3),
            vmem(CHUNKS, rank, l2),
            vmem(CHUNKS, rank, l2),
            vmem(CHUNKS, rank, l1),
            vmem(CHUNKS, rank, l1),
            pltpu.SemaphoreType.DMA((16,)),
            pltpu.SemaphoreType.DMA((64,)),
            pltpu.SemaphoreType.DMA((64,)),
            pltpu.SemaphoreType.DMA((z_count,)),
            pltpu.SemaphoreType.DMA((z_count,)),
        ],
        compiler_params=pltpu.CompilerParams(
            collective_id=0, has_side_effects=True, vmem_limit_bytes=VMEM_LIMIT
        ),
    )(*args)
    return pl.pallas_call(
        finish_kernel,
        name="finish",
        out_shape=jax.ShapeDtypeStruct(shots.shape, f32),
        in_specs=[pl.BlockSpec(memory_space=pltpu.VMEM)] * 3,
        out_specs=pl.BlockSpec(memory_space=pl.ANY),
        scratch_shapes=[vmem(rows, l2), pltpu.SemaphoreType.DMA((4 * CHUNKS,))],
        compiler_params=pltpu.CompilerParams(vmem_limit_bytes=24 * 2**20),
    )(part, w0, leaf_back)


def solution(mesh):
    return jax.shard_map(
        functools.partial(shards, mesh.shape["leaf"]),
        mesh=mesh,
        in_specs=(P("leaf", None),) * 8,
        out_specs=P("leaf", None),
        check_vma=False,
    )
```

profile of v0, /device:TPU:0, one launch (start us, length us, event | category | flops | bytes accessed | tf_op | source)
XLA Modules:
  0.0 66.7 jit_solution(5933606792722420115)
XLA Ops:
  0.0 0.0 copy-start
  0.0 63.1 %solve.1 = (f32[2,2,1024,512]{3,2,1,0:T(8,128)S(1)}, f32[2,2,256,512]{3,2,1,0:T(8,128)S(1)}) custom-call(f32[1024,2048]{1,0:T(8,128)} %shots.1, f32[1024,1024]{1,0:T(8,128)} %leaf_inverse.1, f32[256,1024]{1,0:T(8,128)} %leaf_basis.1, f32[1024,256]{1,0:T(8,128)} %h.1, f32[256,1024]{1,0:T(8,128)} %level_one.1, f32[128,1024]{1,0:T(8,128)} %level_two.1, ...), custom_call_target="tpu_custom_call" | custom-call | tf_op jit(solution)/shard_map/solve/pallas_call | solution.py:405
  63.1 0.0 copy-done
  63.1 3.4 %finish.1 = f32[1024,2048]{1,0:T(8,128)} custom-call(f32[2,2,1024,512]{3,2,1,0:T(8,128)S(1)} %get-tuple-element.7.part, f32[2,2,256,512]{3,2,1,0:T(8,128)S(1)} %get-tuple-element.8.w0, f32[1024,256]{1,0:T(8,128)S(1)} %copy-done), custom_call_target="tpu_custom_call" | custom-call | tf_op jit(solution)/shard_map/finish/pallas_call | solution.py:453
Async XLA Ops:
  0.0 63.1 %copy-start = (f32[1024,256]{1,0:T(8,128)S(1)}, f32[1024,256]{1,0:T(8,128)}, u32[]{:S(2)}) copy-start(f32[1024,256]{1,0:T(8,128)} %h.1) | copy-start | bytes 3145732
where the time goes:
time: 66.8 us; the launch traced here: 66.7 us
  Pallas kernels  66.5 us (100%)
    pallas_call x1, Pallas kernels, shards(): pl.pallas_call(functools.partial(solve_kernel, (n, rank, nodes)), name='s...  63.1 us
    pallas_call x1, Pallas kernels, shards(): pl.pallas_call(finish_kernel, name='finish', out_shape=jax.ShapeDtypeStru...  3.4 us

commit v1 on v0

--- a/solution.py
+++ b/solution.py
@@ -146,6 +146,17 @@
             remote[name + "xy"].start()
             remote[name + "xc"].start()
 
+    for name, buf, slot, rows in (("f3xy", f3, slot3xy, rows3), ("f2x", f2, slot2x, rows2)):
+        view = buf.at[ds(slot, rows), kq]
+        prepare(name + "c", view, view, to_core)
+
+    def forward_kq(condition):
+        @pl.when(condition)
+        def _():
+            for key in ("f3xy", "f2x"):
+                remote[key].wait_recv()
+                remote[key + "c"].start()
+
     local["p"].wait()
     local["e"].wait()
     a0[...] = dot(p[...], e[...])
@@ -166,7 +177,7 @@
             out[c, side, rows, :] = total + dot(e[rows, depth], b[c, side, depth, :])
             return carry
 
-        lax.fori_loop(DEPTHS * first, DEPTHS * last, piece, 0)
+        lax.fori_loop(first, last, piece, 0)
 
     half_leaf = e.shape[0] // 2
 
@@ -176,7 +187,7 @@
     local["f1"].wait()
     arrived("f1")
     g1[...] = dot_t(f1[:, 2 * rank : 3 * rank], f1[:, : 2 * rank])
-    pieces(0, core)
+    pieces(0, 2 * core)
     arrived("f3x")
     forward("f3xy", f3, slot3x, rows3, kq, to_y)
     forward("f3xc", f3, slot3x, rows3, kq, to_core)
@@ -184,33 +195,18 @@
     forward("f3yc", f3, slot3y, rows3, kq, to_core)
     send("ty", top_inverse, top.at[ds(slot3, rows4)], to_y)
     send("f3fy", level_three.at[:, fc], f3.at[ds(slot3, rows3), fc], to_y)
-    pieces(core, 4 * core)
+    pieces(2 * core, 7 * core)
+    forward_kq(core == 1)
     for c in range(CHUNKS):
         arrived(f"c0_{c}")
         product(c1send.at[c], g1, c0[c, :, ds(1 - x, lanes2)])
         for part, half in enumerate((1 - y, y)):
             cols = ds(half, lanes3)
             send(f"c1_{c}{part}", c1send.at[c, :, cols], c1.at[c, ds(x, rank), cols], to_x)
-        if c == 0:
-            remote["tx"].start()
-            remote["fx"].start()
         product(c1.at[c, ds(x, rank)], g1, c0[c, :, ds(x, lanes2)])
+    remote["tx"].start()
+    remote["fx"].start()
     send("f2fx", level_two.at[:, fc], f2.at[ds(slot2, rows2), fc], to_x)
-
-    pieces(4 * core, 3 + core)
-    arrived("f3xy")
-    forward("f3xyc", f3, slot3xy, rows3, kq, to_core)
-    arrived("f2x")
-    forward("f2xc", f2, slot2x, rows2, kq, to_core)
-    z1_piece(0)
-    local["f3"].wait()
-    for name in ("f3c", "f3yc", "f3xc", "f3xyc"):
-        arrived(name)
-    g3[...] = dot_t(f3[:, 2 * rank : 3 * rank], f3[:, : 2 * rank])
-    local["f2"].wait()
-    arrived("f2c")
-    arrived("f2xc")
-    g2[...] = dot_t(f2[:, 2 * rank : 3 * rank], f2[:, : 2 * rank])
 
     def up_two(c, part):
         arrived(f"c1_{c}{part}")
@@ -253,31 +249,44 @@
         for k in to_z:
             guarded(~inner if k == 2 and nodes > 3 else None, block(c, k).wait_recv)
 
+    pieces(7 * core, 6 + core)
+    forward_kq(core == 0)
+    local["f2"].wait()
+    arrived("f2c")
+    arrived("f2xc")
+    g2[...] = dot_t(f2[:, 2 * rank : 3 * rank], f2[:, : 2 * rank])
     up_two(0, 0)
-    pieces(4 * core, 5 * core)
+    local["f3"].wait()
+    for name in ("f3c", "f3yc", "f3xc", "f3xyc"):
+        arrived(name)
+    g3[...] = dot_t(f3[:, 2 * rank : 3 * rank], f3[:, : 2 * rank])
+    z1_piece(0)
+    pieces(7 * core, 9 * core)
     up_two(0, 1)
     product(z2.at[0], f2.at[:, : 2 * rank], c1[0])
     arrived("ty")
     forward("tyc", top, slot3y, rows4, cols4, to_core)
     arrived("f3fy")
     forward("f3fyc", f3, slot3y, rows3, fc, to_core)
-    pieces(3 + 2 * core, 4 + core)
+    pieces(6 + 3 * core, 8 + core)
     up_three(0)
-    forward_late()
     product(z3.at[0], f3.at[:, : 2 * rank], c2[0])
-    pieces(4 + core, 5 + core)
     up_two(1, 0)
     z1_piece(1)
+    up_two(1, 1)
+    pieces(8 + core, 10 + core)
+    forward_late()
+    pass_on(0)
+    up_three(1)
+    product(z3.at[1], f3.at[:, : 2 * rank], c2[1])
+    product(z2.at[1], f2.at[:, : 2 * rank], c1[1])
+    pieces(10 + core, 12 + core)
     arrived("txy")
     forward("txyc", top, slot3xy, rows4, cols4, to_core)
     arrived("fxy")
     forward("fxyc", f3, slot3xy, rows3, fc, to_core)
-    up_two(1, 1)
-    pass_on(0)
-    up_three(1)
-    product(z3.at[1], f3.at[:, : 2 * rank], c2[1])
-    pieces(5 + core, 6)
-    product(z2.at[1], f2.at[:, : 2 * rank], c1[1])
+    arrived("f2fx")
+    forward("f2fxc", f2, slot2x, rows2, fc, to_core)
     local["top"].wait()
     for name in ("tc", "tyc", "txc", "txyc", "f3fyc", "fxc", "fxyc"):
         arrived(name)
@@ -320,17 +329,15 @@
         product(out.at[c, side, :, lanes], h, w0[c, side, :, lanes], out.at[c, side, :, lanes])
 
     down_three(0)
-    arrived("f2fx")
-    forward("f2fxc", f2, slot2x, rows2, fc, to_core)
-    pieces(6, 7)
     arrived("f2fxc")
     down_two(0, 0)
     pass_on(1)
+    pieces(12 + core, 14 + core)
     down_two(0, 1)
     down_one(0, 0)
-    pieces(7, 8)
     down_three(1)
     down_two(1, 0)
+    pieces(14 + core, 16)
     down_one(0, 1)
     local["h"].wait()
     last(0, 0, x)

time: 66.8 us -> 64.7 us (0.969)
  Pallas kernels: 66.5 us -> 64.4 us
    pallas_call x1, Pallas kernels: 63.1 us -> 61 us  [shards(): pl.pallas_call(functools.partial(solve_kernel, (n, rank, nodes)), name='s...]
where the time goes in v1:
time: 64.7 us; the launch traced here: 64.6 us
  Pallas kernels  64.4 us (100%)
    pallas_call x1, Pallas kernels, shards(): pl.pallas_call(functools.partial(solve_kernel, (n, rank, nodes)), name='s...  61 us
    pallas_call x1, Pallas kernels, shards(): pl.pallas_call(finish_kernel, name='finish', out_shape=jax.ShapeDtypeStru...  3.4 us

profile of v1, /device:TPU:0, one launch (start us, length us, event | category | flops | bytes accessed | tf_op | source)
XLA Modules:
  0.0 64.6 jit_solution(13518960544501961233)
XLA Ops:
  0.0 0.0 copy-start
  0.0 61.0 %solve.1 = (f32[2,2,1024,512]{3,2,1,0:T(8,128)S(1)}, f32[2,2,256,512]{3,2,1,0:T(8,128)S(1)}) custom-call(f32[1024,2048]{1,0:T(8,128)} %shots.1, f32[1024,1024]{1,0:T(8,128)} %leaf_inverse.1, f32[256,1024]{1,0:T(8,128)} %leaf_basis.1, f32[1024,256]{1,0:T(8,128)} %h.1, f32[256,1024]{1,0:T(8,128)} %level_one.1, f32[128,1024]{1,0:T(8,128)} %level_two.1, ...), custom_call_target="tpu_custom_call" | custom-call | tf_op jit(solution)/shard_map/solve/pallas_call | solution.py:412
  61.0 0.0 copy-done
  61.0 3.4 %finish.1 = f32[1024,2048]{1,0:T(8,128)} custom-call(f32[2,2,1024,512]{3,2,1,0:T(8,128)S(1)} %get-tuple-element.7.part, f32[2,2,256,512]{3,2,1,0:T(8,128)S(1)} %get-tuple-element.8.w0, f32[1024,256]{1,0:T(8,128)S(1)} %copy-done), custom_call_target="tpu_custom_call" | custom-call | tf_op jit(solution)/shard_map/finish/pallas_call | solution.py:460
Async XLA Ops:
  0.0 61.0 %copy-start = (f32[1024,256]{1,0:T(8,128)S(1)}, f32[1024,256]{1,0:T(8,128)}, u32[]{:S(2)}) copy-start(f32[1024,256]{1,0:T(8,128)} %h.1) | copy-start | bytes 3145732

commit v2 on v1

--- a/solution.py
+++ b/solution.py
@@ -140,8 +140,8 @@
         prepare(name + "xy", view, view, to_y)
         prepare(name + "xc", view, view, to_core)
 
-    def forward_late():
-        for name in "tf":
+    def forward_late(names):
+        for name in names:
             remote[name + "x"].wait_recv()
             remote[name + "xy"].start()
             remote[name + "xc"].start()
@@ -202,10 +202,11 @@
         product(c1send.at[c], g1, c0[c, :, ds(1 - x, lanes2)])
         for part, half in enumerate((1 - y, y)):
             cols = ds(half, lanes3)
+            if (c, part) == (CHUNKS - 1, 1):
+                remote["tx"].start()
+                remote["fx"].start()
             send(f"c1_{c}{part}", c1send.at[c, :, cols], c1.at[c, ds(x, rank), cols], to_x)
         product(c1.at[c, ds(x, rank)], g1, c0[c, :, ds(x, lanes2)])
-    remote["tx"].start()
-    remote["fx"].start()
     send("f2fx", level_two.at[:, fc], f2.at[ds(slot2, rows2), fc], to_x)
 
     def up_two(c, part):
@@ -255,32 +256,32 @@
     arrived("f2c")
     arrived("f2xc")
     g2[...] = dot_t(f2[:, 2 * rank : 3 * rank], f2[:, : 2 * rank])
+    pieces(7 * core, 9 * core)
     up_two(0, 0)
     local["f3"].wait()
     for name in ("f3c", "f3yc", "f3xc", "f3xyc"):
         arrived(name)
     g3[...] = dot_t(f3[:, 2 * rank : 3 * rank], f3[:, : 2 * rank])
     z1_piece(0)
-    pieces(7 * core, 9 * core)
     up_two(0, 1)
     product(z2.at[0], f2.at[:, : 2 * rank], c1[0])
     arrived("ty")
     forward("tyc", top, slot3y, rows4, cols4, to_core)
     arrived("f3fy")
     forward("f3fyc", f3, slot3y, rows3, fc, to_core)
-    pieces(6 + 3 * core, 8 + core)
+    pieces(6 + 3 * core, 7 + 2 * core)
     up_three(0)
     product(z3.at[0], f3.at[:, : 2 * rank], c2[0])
     up_two(1, 0)
     z1_piece(1)
+    pieces(7 + 2 * core, 9 + core)
+    forward_late("tf")
     up_two(1, 1)
-    pieces(8 + core, 10 + core)
-    forward_late()
     pass_on(0)
     up_three(1)
     product(z3.at[1], f3.at[:, : 2 * rank], c2[1])
     product(z2.at[1], f2.at[:, : 2 * rank], c1[1])
-    pieces(10 + core, 12 + core)
+    pieces(9 + core, 11 - core)
     arrived("txy")
     forward("txyc", top, slot3xy, rows4, cols4, to_core)
     arrived("fxy")
@@ -328,29 +329,28 @@
         lanes = ds(half, lanes2)
         product(out.at[c, side, :, lanes], h, w0[c, side, :, lanes], out.at[c, side, :, lanes])
 
+    pieces(11 - core, 11 + core)
     down_three(0)
     arrived("f2fxc")
     down_two(0, 0)
     pass_on(1)
-    pieces(12 + core, 14 + core)
+    pieces(11 + core, 13 + core)
     down_two(0, 1)
     down_one(0, 0)
     down_three(1)
     down_two(1, 0)
-    pieces(14 + core, 16)
+    pieces(13 + core, 16)
     down_one(0, 1)
     local["h"].wait()
-    last(0, 0, x)
     down_two(1, 1)
     down_one(1, 0)
-    last(0, 0, 1 - x)
+    out[0, 0] = out[0, 0] - dot(h[...], w0[0, 0])
+    last(1, 0, x)
     arrived("w0_00")
-    last(0, 1, x)
-    last(1, 0, x)
+    arrived("w0_01")
+    out[0, 1] = out[0, 1] - dot(h[...], w0[0, 1])
     arrived("w0_10")
     last(1, 1, x)
-    arrived("w0_01")
-    last(0, 1, 1 - x)
     down_one(1, 1)
     last(1, 0, 1 - x)
     arrived("w0_11")

time: 64.7 us -> 64.5 us (level)
  no operation moved by 1% of the time
where the time goes in v2:
time: 64.5 us; the launch traced here: 64.4 us
  Pallas kernels  64.2 us (100%)
    pallas_call x1, Pallas kernels, shards(): pl.pallas_call(functools.partial(solve_kernel, (n, rank, nodes)), name='s...  60.8 us
    pallas_call x1, Pallas kernels, shards(): pl.pallas_call(finish_kernel, name='finish', out_shape=jax.ShapeDtypeStru...  3.4 us

profile of v2, /device:TPU:0, one launch (start us, length us, event | category | flops | bytes accessed | tf_op | source)
XLA Modules:
  0.0 64.4 jit_solution(9520132440024291803)
XLA Ops:
  0.0 0.0 copy-start
  0.0 60.8 %solve.1 = (f32[2,2,1024,512]{3,2,1,0:T(8,128)S(1)}, f32[2,2,256,512]{3,2,1,0:T(8,128)S(1)}) custom-call(f32[1024,2048]{1,0:T(8,128)} %shots.1, f32[1024,1024]{1,0:T(8,128)} %leaf_inverse.1, f32[256,1024]{1,0:T(8,128)} %leaf_basis.1, f32[1024,256]{1,0:T(8,128)} %h.1, f32[256,1024]{1,0:T(8,128)} %level_one.1, f32[128,1024]{1,0:T(8,128)} %level_two.1, ...), custom_call_target="tpu_custom_call" | custom-call | tf_op jit(solution)/shard_map/solve/pallas_call | solution.py:412
  60.8 0.0 copy-done
  60.8 3.4 %finish.1 = f32[1024,2048]{1,0:T(8,128)} custom-call(f32[2,2,1024,512]{3,2,1,0:T(8,128)S(1)} %get-tuple-element.7.part, f32[2,2,256,512]{3,2,1,0:T(8,128)S(1)} %get-tuple-element.8.w0, f32[1024,256]{1,0:T(8,128)S(1)} %copy-done), custom_call_target="tpu_custom_call" | custom-call | tf_op jit(solution)/shard_map/finish/pallas_call | solution.py:460
Async XLA Ops:
  0.0 60.8 %copy-start = (f32[1024,256]{1,0:T(8,128)S(1)}, f32[1024,256]{1,0:T(8,128)}, u32[]{:S(2)}) copy-start(f32[1024,256]{1,0:T(8,128)} %h.1) | copy-start | bytes 3145732

commit v3 on v2

--- a/solution.py
+++ b/solution.py
@@ -10,6 +10,7 @@
 LEVELS = 3
 CHUNKS = 2
 DEPTHS = 2
+LOCALS, REMOTES = 11, 44
 HIGH = lax.Precision.HIGH
 MESH = pl.DeviceIdType.MESH
 VMEM_LIMIT = 48 * 2**20
@@ -83,6 +84,22 @@
         half = core if side == 0 else 1 - core
         return ds(c * 2 + half, lanes1)
 
+    barrier = pltpu.get_barrier_semaphore()
+
+    def between(k):
+        return inner if k == 3 else None
+
+    def guarded(condition, action):
+        action() if condition is None else pl.when(condition)(action)
+
+    def greet(peer):
+        pl.semaphore_signal(barrier, inc=1, device_id=(peer,), device_id_type=MESH)
+
+    for peer in (to_core, to_x, to_y):
+        greet(peer)
+    for k, peer in to_z.items():
+        guarded(between(k), functools.partial(greet, peer))
+    far = 1 - inner.astype(jnp.int32) if nodes > 3 else 0
     load("p", leaf_basis, p)
     load("e", leaf_inverse, e)
     load("b01", shots.at[:, columns(0, 1)], b.at[0, 1])
@@ -97,32 +114,16 @@
     load("top", top_inverse, top.at[ds(slot3, rows4)])
     load("h", leaf_back, h)
 
-    barrier = pltpu.get_barrier_semaphore()
-
-    def between(k):
-        return inner if k == 3 else None
-
-    def guarded(condition, action):
-        action() if condition is None else pl.when(condition)(action)
-
-    def greet(peer):
-        pl.semaphore_signal(barrier, inc=1, device_id=(peer,), device_id_type=MESH)
-
-    for peer in (to_core, to_x, to_y):
-        greet(peer)
-    for k, peer in to_z.items():
-        guarded(between(k), functools.partial(greet, peer))
-    far = 1 - inner.astype(jnp.int32) if nodes > 3 else 0
     pl.semaphore_wait(barrier, 3 + len(to_z) - far)
 
     kq, fc = pl.ds(0, 3 * rank), pl.ds(3 * rank, rank)
     slot2x = (1 - x) * 2 + core
     slot3x, slot3y = y * 4 + (1 - x) * 2 + core, (1 - y) * 4 + x * 2 + core
     slot3xy = (1 - y) * 4 + (1 - x) * 2 + core
-    send("f1", level_one, f1.at[ds(core, rows1)], to_core)
-    send("f3y", level_three.at[:, kq], f3.at[ds(slot3, rows3), kq], to_y)
     send("f3x", level_three.at[:, kq], f3.at[ds(slot3, rows3), kq], to_x)
     send("f2x", level_two.at[:, kq], f2.at[ds(slot2, rows2), kq], to_x)
+    send("f3y", level_three.at[:, kq], f3.at[ds(slot3, rows3), kq], to_y)
+    send("f1", level_one, f1.at[ds(core, rows1)], to_core)
     send("f2c", level_two, f2.at[ds(slot2, rows2)], to_core)
     send("f3c", level_three, f3.at[ds(slot3, rows3)], to_core)
     send("tc", top_inverse, top.at[ds(slot3, rows4)], to_core)
@@ -325,6 +326,18 @@
         send(f"w0_{c}{part}", w0send.at[c, :, lanes], w0.at[c, 1, :, lanes], to_core)
         product(w0.at[c, 0, :, lanes], f1.at[own, 3 * rank :], w1[c, :, lanes], z1.at[c, own, lanes])
 
+    def drain(chosen):
+        for name, copy in remote.items():
+            if chosen(name):
+                copy.wait_send()
+
+    def drain_nodes():
+        for c in range(CHUNKS):
+            for k in to_z:
+                guarded(between(k), block(c, k).wait_send)
+            if nodes > 3:
+                pl.when(inner)(passed(c).wait_send)
+
     def last(c, side, half):
         lanes = ds(half, lanes2)
         product(out.at[c, side, :, lanes], h, w0[c, side, :, lanes], out.at[c, side, :, lanes])
@@ -335,11 +348,13 @@
     down_two(0, 0)
     pass_on(1)
     pieces(11 + core, 13 + core)
+    drain(lambda name: name[0] != "w")
     down_two(0, 1)
     down_one(0, 0)
     down_three(1)
     down_two(1, 0)
     pieces(13 + core, 16)
+    drain_nodes()
     down_one(0, 1)
     local["h"].wait()
     down_two(1, 1)
@@ -354,13 +369,8 @@
     down_one(1, 1)
     last(1, 0, 1 - x)
     arrived("w0_11")
-    for copy in remote.values():
-        copy.wait_send()
-    for c in range(CHUNKS):
-        for k in to_z:
-            guarded(between(k), block(c, k).wait_send)
-        if nodes > 3:
-            pl.when(inner)(passed(c).wait_send)
+    drain(lambda name: name[0] == "w")
+    assert (len(local), len(remote)) == (LOCALS, REMOTES)
 
 
 def flip_of(value, mask):
@@ -447,9 +457,9 @@
             vmem(CHUNKS, rank, l2),
             vmem(CHUNKS, rank, l1),
             vmem(CHUNKS, rank, l1),
-            pltpu.SemaphoreType.DMA((16,)),
-            pltpu.SemaphoreType.DMA((64,)),
-            pltpu.SemaphoreType.DMA((64,)),
+            pltpu.SemaphoreType.DMA((LOCALS,)),
+            pltpu.SemaphoreType.DMA((REMOTES,)),
+            pltpu.SemaphoreType.DMA((REMOTES,)),
             pltpu.SemaphoreType.DMA((z_count,)),
             pltpu.SemaphoreType.DMA((z_count,)),
         ],

time: 64.5 us -> 63.8 us (0.989)
  Pallas kernels: 64.2 us -> 63.5 us
    pallas_call x1, Pallas kernels: 60.8 us -> 60.1 us  [shards(): pl.pallas_call(functools.partial(solve_kernel, (n, rank, nodes)), name='s...]
where the time goes in v3:
time: 63.8 us; the launch traced here: 63.7 us
  Pallas kernels  63.5 us (100%)
    pallas_call x1, Pallas kernels, shards(): pl.pallas_call(functools.partial(solve_kernel, (n, rank, nodes)), name='s...  60.1 us
    pallas_call x1, Pallas kernels, shards(): pl.pallas_call(finish_kernel, name='finish', out_shape=jax.ShapeDtypeStru...  3.4 us

profile of v3, /device:TPU:0, one launch (start us, length us, event | category | flops | bytes accessed | tf_op | source)
XLA Modules:
  0.0 63.7 jit_solution(14098783245821105380)
XLA Ops:
  0.0 0.0 copy-start
  0.0 60.1 %solve.1 = (f32[2,2,1024,512]{3,2,1,0:T(8,128)S(1)}, f32[2,2,256,512]{3,2,1,0:T(8,128)S(1)}) custom-call(f32[1024,2048]{1,0:T(8,128)} %shots.1, f32[1024,1024]{1,0:T(8,128)} %leaf_inverse.1, f32[256,1024]{1,0:T(8,128)} %leaf_basis.1, f32[1024,256]{1,0:T(8,128)} %h.1, f32[256,1024]{1,0:T(8,128)} %level_one.1, f32[128,1024]{1,0:T(8,128)} %level_two.1, ...), custom_call_target="tpu_custom_call" | custom-call | tf_op jit(solution)/shard_map/solve/pallas_call | solution.py:422
  60.1 0.0 copy-done
  60.1 3.4 %finish.1 = f32[1024,2048]{1,0:T(8,128)} custom-call(f32[2,2,1024,512]{3,2,1,0:T(8,128)S(1)} %get-tuple-element.7.part, f32[2,2,256,512]{3,2,1,0:T(8,128)S(1)} %get-tuple-element.8.w0, f32[1024,256]{1,0:T(8,128)S(1)} %copy-done), custom_call_target="tpu_custom_call" | custom-call | tf_op jit(solution)/shard_map/finish/pallas_call | solution.py:470
Async XLA Ops:
  0.0 60.1 %copy-start = (f32[1024,256]{1,0:T(8,128)S(1)}, f32[1024,256]{1,0:T(8,128)}, u32[]{:S(2)}) copy-start(f32[1024,256]{1,0:T(8,128)} %h.1) | copy-start | bytes 3145732
